TPU v7x, 32 devices: a whole 2x2x4 slice. The times are simulated.
32 devices in a mesh: group: 2 (over x), dp: 4 (over y, core), tensor: 4 (over z).
Axes of the slice: x: 2, y: 2, z: 4, core: 2. Of those that a mesh axis runs over, the one named last changes fastest.
Arguments:
- tokens: bfloat16 [1024, 5120], P(('group', 'dp'), 'tensor'), parts along dimension 0, may hold values from -6 to 6
- router: bfloat16 [5120, 2], replicated, may hold values from -0.078125 to 0.078125
- expert_gate: bfloat16 [5120, 8192], P(None, ('dp', 'tensor')), may hold values from -0.078125 to 0.078125
- expert_up: bfloat16 [5120, 8192], P(None, ('dp', 'tensor')), may hold values from -0.078125 to 0.078125
- expert_down: bfloat16 [8192, 5120], P(('dp', 'tensor')), may hold values from -0.09375 to 0.09375
- shared_gate: bfloat16 [5120, 4096], P('dp', 'tensor'), may hold values from -0.078125 to 0.078125
- shared_up: bfloat16 [5120, 4096], P('dp', 'tensor'), may hold values from -0.078125 to 0.078125
- shared_down: bfloat16 [4096, 5120], P('tensor', 'dp'), may hold values from -0.09375 to 0.09375
- expert_ids: int32 [1024], P(('group', 'dp')), parts along dimension 0, may hold values from 0 to 1, as said below
- expert_slots: int32 [1024], P(('group', 'dp')), parts along dimension 0, may hold values from 0 to 63, as said below
Outputs:
- mixed: bfloat16 [1024, 5120], P(('group', 'dp'), 'tensor'), parts along dimension 0
There are 2 independent parts, one for each index of `group`. A program takes and returns all parts, laid end to end along the dimension named above; an argument that names none is the same for every part. Nothing has to cross between parts.
Inputs may be any that keep to these rules, and one draw needn't show every extreme that they name: `expert_ids`: among the tokens of one index of dp no expert has more than 64; in every draw one expert has exactly 64 tokens from every index of dp. `expert_slots`: tokens of one index of dp with the same expert have distinct slots.
All inputs are finite; a program needn't handle non-finite values.
Results may differ from a plain program's by a relative error of at most 0.015.
Values may be sent and summed in bfloat16 or wider, within the bound.
A program may use at most 128 MiB of HBM per device.

v0:
```python
import jax
import jax.numpy as jnp
from jax import lax
from jax.sharding import PartitionSpec as P


def on_device(
    tokens,
    router,
    expert_gate,
    expert_up,
    expert_down,
    shared_gate,
    shared_up,
    shared_down,
    expert_ids,
    expert_slots,
):
    tok_rows, part_width = tokens.shape
    dp_count = lax.axis_size("dp")
    experts = dp_count // 2
    capacity = min(2 * tok_rows // experts, tok_rows // 2)
    gathered = lax.all_gather(tokens, "tensor", axis=1, tiled=True)
    logits = jnp.dot(gathered, router, preferred_element_type=jnp.float32)
    one_hot = (expert_ids[:, None] == jnp.arange(experts, dtype=jnp.int32)[None, :]).astype(
        jnp.float32
    )
    gating = jax.nn.sigmoid(jnp.sum(logits * one_hot, axis=1))
    routed = (tokens.astype(jnp.float32) * gating[:, None]).astype(jnp.bfloat16)
    outgoing = (
        jnp.zeros((experts, capacity, part_width), jnp.bfloat16)
        .at[expert_ids, expert_slots]
        .set(routed)
    )
    gate_sum = jnp.dot(
        gathered,
        lax.all_gather(shared_gate, "dp", axis=0, tiled=True),
        preferred_element_type=jnp.float32,
    )
    up_sum = jnp.dot(
        gathered,
        lax.all_gather(shared_up, "dp", axis=0, tiled=True),
        preferred_element_type=jnp.float32,
    )
    shared_hidden = (jax.nn.silu(gate_sum) * up_sum).astype(jnp.bfloat16)
    shared_terms = jnp.dot(
        shared_hidden,
        lax.all_gather(shared_down, "dp", axis=1, tiled=True),
        preferred_element_type=jnp.float32,
    )
    shared_out = lax.psum_scatter(
        shared_terms.astype(jnp.bfloat16), "tensor", scatter_dimension=1, tiled=True
    ).astype(jnp.float32)
    to_send = jnp.repeat(outgoing, 2, axis=0)
    received = lax.all_to_all(to_send, "dp", split_axis=0, concat_axis=0, tiled=True)
    source_count = received.shape[0]
    slot_count = received.shape[1]
    slot_total = source_count * slot_count
    portion = lax.all_gather(received, "tensor", axis=2, tiled=True)
    flattened = portion.reshape(slot_total, portion.shape[2])
    gate_e = jnp.dot(flattened, expert_gate, preferred_element_type=jnp.float32)
    up_e = jnp.dot(flattened, expert_up, preferred_element_type=jnp.float32)
    hidden_e = (jax.nn.silu(gate_e) * up_e).astype(jnp.bfloat16)
    expert_terms = jnp.dot(hidden_e, expert_down, preferred_element_type=jnp.float32)
    expert_terms = expert_terms.reshape(source_count, slot_count, expert_terms.shape[1])
    returned_raw = lax.all_to_all(
        lax.psum_scatter(
            expert_terms.astype(jnp.bfloat16), "tensor", scatter_dimension=2, tiled=True
        ),
        "dp",
        split_axis=0,
        concat_axis=0,
        tiled=True,
    ).astype(jnp.float32)
    returned = (
        returned_raw.reshape(experts, 2, capacity, part_width).sum(axis=1).astype(jnp.bfloat16)
    )
    expert_out = returned[expert_ids, expert_slots]
    return (shared_out + expert_out.astype(jnp.float32)).astype(jnp.bfloat16)


def solution(mesh):
    in_specs = (
        P(("group", "dp"), "tensor"),
        P(),
        P(None, ("dp", "tensor")),
        P(None, ("dp", "tensor")),
        P(("dp", "tensor"), None),
        P("dp", "tensor"),
        P("dp", "tensor"),
        P("tensor", "dp"),
        P(("group", "dp")),
        P(("group", "dp")),
    )
    out_specs = P(("group", "dp"), "tensor")
    return jax.shard_map(
        on_device, mesh=mesh, in_specs=in_specs, out_specs=out_specs, check_vma=False
    )
```

profile of v0, /device:TPU:0, one launch (start us, length us, event | category | flops | bytes accessed | tf_op | source)
XLA Modules:
  0.0 433.6 jit_solution(5085881878389791169)
XLA Ops:
  6.5 0.7 all-gather.6.cloned.1.call-update
  7.3 0.0 all-gather.14.cloned.1.call-start
  7.3 0.7 fusion.19
  8.0 36.2 %all-gather.6.cloned.1.call-done = bf16[128,5120]{1,0:T(8,128)(2,1)} async-done(((bf16[128,1280]{1,0:T(8,128)(2,1)}), bf16[128,5120]{1,0:T(8,128)(2,1)}) %all-gather.6.cloned.1.call-update) | async-done | bytes 1310736 | tf_op jit(solution)/shard_map/all_gather | solution.py:23
  44.2 1.8 fusion.2
  46.0 1.1 multiply_convert_fusion
  47.1 9.8 %scatter_fusion = bf16[2,64,1280]{2,1,0:T(8,128)(2,1)S(1)} fusion(bf16[2,64,1280]{2,1,0:T(8,128)(2,1)S(1)} %broadcast_in_dim.8, s32[128]{0:T(128)S(1)} %get-tuple-element.6, bf16[128,1280]{1,0:T(8,128)(2,1)S(1)} %multiply_convert_fusion), kind=kCustom, calls=%fused_computation.1 | custom fusion | bytes 984064 | tf_op jit(solution)/shard_map/scatter | solution.py:33
  57.0 13.3 %all_to_all.10 = bf16[4,64,1280]{2,1,0:T(8,128)(2,1)} all-to-all(bf16[4,64,1280]{2,1,0:T(8,128)(2,1)S(1)} %bitcast.42), channel_id=1, replica_groups=mesh['group'=2,'dp'=4,'tensor'=4] {'dp'}, dimensions={0} | all-to-all | bytes 1310720 | tf_op jit(solution)/shard_map/all_to_all | solution.py:55
  70.3 0.0 all-gather.14.cloned.1.call-update
  70.4 0.0 all-gather.8.cloned.1.call-start
  70.4 0.7 all-gather.8.cloned.1.call-update
  71.1 0.0 all-gather.10.cloned.1.call-start
  71.1 0.5 all-gather.10.cloned.1.call-update
  71.7 0.0 all-gather.12.cloned.1.call-start
  71.7 0.5 all-gather.12.cloned.1.call-update
  72.3 0.0 reduce-scatter.5.cloned.1.call-start
  72.3 51.1 %all-gather.14.cloned.1.call-done = bf16[4,64,5120]{2,1,0:T(8,128)(2,1)} async-done(((bf16[4,64,1280]{2,1,0:T(8,128)(2,1)}), bf16[4,64,5120]{2,1,0:T(8,128)(2,1)}) %all-gather.14.cloned.1.call-update) | async-done | bytes 2621456 | tf_op jit(solution)/shard_map/all_gather | solution.py:59
  123.5 4.8 %fusion.23 = f32[256,512]{1,0:T(8,128)S(1)} fusion(bf16[256,5120]{1,0:T(8,128)(2,1)} %bitcast.43, bf16[5120,512]{1,0:T(8,128)(2,1)} %param.12), kind=kOutput, calls=%fused_computation.39 | convolution fusion | flops 1342177280 | bytes 8388608 | tf_op jit(solution)/shard_map/dot_general | solution.py:61
  128.3 11.2 %convolution_convert_fusion = bf16[256,5120]{1,0:T(8,128)(2,1)} fusion(bf16[512,5120]{1,0:T(8,128)(2,1)} %param.14, bf16[256,5120]{1,0:T(8,128)(2,1)} %bitcast.44, bf16[5120,512]{1,0:T(8,128)(2,1)} %param.13, f32[256,512]{1,0:T(8,128)S(1)} %fusion.23), kind=kOutput, calls=%fused_computation.2 | convolution fusion | flops 2686451712 | bytes 16252928 | tf_op jit(solution)/shard_map/dot_general | solution.py:64
  139.4 0.0 reduce-scatter.5.cloned.1.call-update
  139.5 0.0 reduce-scatter.3.cloned.1.call-start
  139.5 54.5 %all-gather.8.cloned.1.call-done = bf16[5120,1024]{1,0:T(8,128)(2,1)} async-done(((bf16[1280,1024]{1,0:T(8,128)(2,1)}), bf16[5120,1024]{1,0:T(8,128)(2,1)}) %all-gather.8.cloned.1.call-update) | async-done | bytes 10485776 | tf_op jit(solution)/shard_map/all_gather | solution.py:37
  194.0 5.6 %fusion.22 = f32[128,1024]{1,0:T(8,128)S(1)} fusion(bf16[128,5120]{1,0:T(8,128)(2,1)S(1)} %copy-done.2, bf16[5120,1024]{1,0:T(8,128)(2,1)} %all-gather.8.cloned.1.call-done), kind=kOutput, calls=%fused_computation.38 | convolution fusion | flops 1342177280 | bytes 12320768 | tf_op jit(solution)/shard_map/dot_general | solution.py:35
  199.6 66.0 %all-gather.10.cloned.1.call-done = bf16[5120,1024]{1,0:T(8,128)(2,1)} async-done(((bf16[1280,1024]{1,0:T(8,128)(2,1)}), bf16[5120,1024]{1,0:T(8,128)(2,1)}) %all-gather.10.cloned.1.call-update) | async-done | bytes 10485776 | tf_op jit(solution)/shard_map/all_gather | solution.py:42
  265.6 71.6 %all-gather.12.cloned.1.call-done = bf16[1024,5120]{1,0:T(8,128)(2,1)} async-done(((bf16[1024,1280]{1,0:T(8,128)(2,1)}), bf16[1024,5120]{1,0:T(8,128)(2,1)}) %all-gather.12.cloned.1.call-update) | async-done | bytes 10485776 | tf_op jit(solution)/shard_map/all_gather | solution.py:48
  337.2 11.2 %convolution_convert_fusion.1 = bf16[128,5120]{1,0:T(8,128)(2,1)} fusion(bf16[1024,5120]{1,0:T(8,128)(2,1)} %all-gather.12.cloned.1.call-done, bf16[128,5120]{1,0:T(8,128)(2,1)S(1)} %copy-done.2, bf16[5120,1024]{1,0:T(8,128)(2,1)} %all-gather.10.cloned.1.call-done, f32[128,1024]{1,0:T(8,128)S(1)} %fusion.22), kind=kOutput, calls=%fused_computation.3 | convolution fusion | flops 2685796352 | bytes 24117248 | tf_op jit(solution)/shard_map/dot_general | solution.py:46
  348.5 43.2 %reduce-scatter.5.cloned.1.call-done = bf16[4,64,1280]{2,1,0:T(8,128)(2,1)} async-done(((bf16[4,64,5120]{2,1,0:T(8,128)(2,1)}), bf16[4,64,1280]{2,1,0:T(8,128)(2,1)}) %reduce-scatter.5.cloned.1.call-update) | async-done | bytes 655376 | tf_op jit(solution)/shard_map/reduce_scatter | solution.py:67
  391.7 13.7 %all_to_all.11 = bf16[4,64,1280]{2,1,0:T(8,128)(2,1)S(1)} all-to-all(bf16[4,64,1280]{2,1,0:T(8,128)(2,1)} %reduce-scatter.5.cloned.1.call-done), channel_id=1, replica_groups=mesh['group'=2,'dp'=4,'tensor'=4] {'dp'}, dimensions={0} | all-to-all | bytes 1310720 | tf_op jit(solution)/shard_map/all_to_all | solution.py:66
  405.3 0.1 bitcast_reduce_fusion
  405.4 1.9 gather_fusion
  407.3 17.6 %reduce-scatter.3.cloned.1.call-done = bf16[128,1280]{1,0:T(8,128)(2,1)} async-done(((bf16[128,5120]{1,0:T(8,128)(2,1)}), bf16[128,1280]{1,0:T(8,128)(2,1)}) %reduce-scatter.3.cloned.1.call-update) | async-done | bytes 327696 | tf_op jit(solution)/shard_map/reduce_scatter | solution.py:51
  424.9 1.8 add_convert_fusion
  (11 shorter events, 0.1 us)
Async XLA Ops:
  6.5 37.6 %copy-start = (bf16[5120,2]{0,1:T(2,128)(2,1)S(1)}, bf16[5120,2]{0,1:T(2,128)(2,1)}, u32[]{:S(2)}) copy-start(bf16[5120,2]{0,1:T(2,128)(2,1)} %param.11) | copy-start | bytes 61444
  6.5 37.6 %all-gather.6.cloned.1.call-start = ((), (), s32[]{:S(2)}) async-start(), calls=%async_computation.4 | async-start | bytes 1638400 | tf_op jit(solution)/shard_map/all_gather | solution.py:23
  7.3 116.2 %all-gather.14.cloned.1.call-start = ((), (), s32[]{:S(2)}) async-start(), calls=%async_computation.9 | async-start | bytes 3276800 | tf_op jit(solution)/shard_map/all_gather | solution.py:59
  70.4 123.6 %all-gather.8.cloned.1.call-start = ((), (), s32[]{:S(2)}) async-start(), calls=%async_computation.5 | async-start | bytes 13107200 | tf_op jit(solution)/shard_map/all_gather | solution.py:37
  71.1 194.5 %all-gather.10.cloned.1.call-start = ((), (), s32[]{:S(2)}) async-start(), calls=%async_computation.6 | async-start | bytes 13107200 | tf_op jit(solution)/shard_map/all_gather | solution.py:42
  71.7 265.6 %all-gather.12.cloned.1.call-start = ((), (), s32[]{:S(2)}) async-start(), calls=%async_computation.7 | async-start | bytes 13107200 | tf_op jit(solution)/shard_map/all_gather | solution.py:48
  72.3 319.4 %reduce-scatter.5.cloned.1.call-start = ((), (), s32[]{:S(2)}) async-start(), calls=%async_computation.10 | async-start | bytes 3276800 | tf_op jit(solution)/shard_map/reduce_scatter | solution.py:67
  128.3 65.7 %copy-start.2 = (bf16[128,5120]{1,0:T(8,128)(2,1)S(1)}, bf16[128,5120]{1,0:T(8,128)(2,1)}, u32[]{:S(2)}) copy-start(bf16[128,5120]{1,0:T(8,128)(2,1)} %all-gather.6.cloned.1.call-done) | copy-start | bytes 3932164
  139.5 285.5 %reduce-scatter.3.cloned.1.call-start = ((), (), s32[]{:S(2)}) async-start(), calls=%async_computation.8 | async-start | bytes 1638400 | tf_op jit(solution)/shard_map/reduce_scatter | solution.py:51
  337.2 89.5 %copy-start.1 = (bf16[5120,2]{0,1:T(2,128)(2,1)S(1)}, bf16[5120,2]{0,1:T(2,128)(2,1)}, u32[]{:S(2)}) copy-start(bf16[5120,2]{0,1:T(2,128)(2,1)} %param.11) | copy-start | bytes 61444
Sparse Core Ops, SparseCore 0:
  8.9 35.2 all-gather.5
  70.5 52.9 all-gather.13
  125.0 68.9 all-gather.7
  195.4 70.1 all-gather.9
  267.0 70.1 all-gather.11
  339.4 52.2 reduce-scatter.4
  394.0 30.9 reduce-scatter.2
where the time goes:
time: 434 us
  waiting for transfers between devices  343 us (79%)
  matrix products  34.5 us (8%)
  blocking collectives  27 us (6%)
  between operations  13.6 us (3%)
  local copies, waits for them, and re-layouts  11.8 us (3%)
    all_gather x1, waiting for transfers between devices, on_device(): lax.all_gather(shared_down, 'dp', axis=1, tiled=True)  71.6 us
    all_gather x1, waiting for transfers between devices, on_device(): lax.all_gather(shared_up, 'dp', axis=0, tiled=True)  66 us
    all_gather x1, waiting for transfers between devices, on_device(): lax.all_gather(shared_gate, 'dp', axis=0, tiled=True)  54.5 us
    all_gather x1, waiting for transfers between devices, on_device(): portion = lax.all_gather(received, 'tensor', axis=2, tiled=True)  51.1 us
    reduce_scatter x1, waiting for transfers between devices, on_device(): lax.psum_scatter(expert_terms.astype(jnp.bfloat16), 'tensor', scatter_dim...  43.2 us
    all_gather x1, waiting for transfers between devices, on_device(): gathered = lax.all_gather(tokens, 'tensor', axis=1, tiled=True)  36.2 us
    reduce_scatter x1, waiting for transfers between devices, on_device(): lax.psum_scatter(shared_terms.astype(jnp.bfloat16), 'tensor', scatter_dim...  17.6 us
    all_to_all x1, blocking collectives, on_device(): lax.all_to_all(lax.psum_scatter(expert_terms.astype(jnp.bfloat16), 'tenso...  13.7 us
  transfers between devices with their start and end apart: 7, of which 7 were waited for; matrix products, arithmetic and copies ran while one was open for 8% of the time, Pallas kernels for 0%

commit v1 on v0

--- a/solution.py
+++ b/solution.py
@@ -56,7 +56,14 @@
     source_count = received.shape[0]
     slot_count = received.shape[1]
     slot_total = source_count * slot_count
-    portion = lax.all_gather(received, "tensor", axis=2, tiled=True)
+    ring = [received]
+    for hop in range(3):
+        ring.append(lax.ppermute(ring[-1], "tensor", [(dev, (dev + 1) % 4) for dev in range(4)]))
+    portion = jnp.roll(
+        jnp.concatenate(ring[::-1], axis=2),
+        (lax.axis_index("tensor") + 1) * ring[0].shape[2],
+        axis=2,
+    )
     flattened = portion.reshape(slot_total, portion.shape[2])
     gate_e = jnp.dot(flattened, expert_gate, preferred_element_type=jnp.float32)
     up_e = jnp.dot(flattened, expert_up, preferred_element_type=jnp.float32)

time: 434 us -> 362 us (0.83)
  waiting for transfers between devices: 343 us -> 264 us
  blocking collectives: 27 us -> 33.9 us
    all_gather x1, waiting for transfers between devices: 54.5 us -> 0.02 us  [on_device(): lax.all_gather(shared_gate, 'dp', axis=0, tiled=True)]
    all_gather x1 -> x0, waiting for transfers between devices: 51.1 us -> none  [on_device(): portion = lax.all_gather(received, 'tensor', axis=2, tiled=True)]
    ppermute x0 -> x3, waiting for transfers between devices: none -> 51.1 us  [on_device(): lax.ppermute(ring[-1], 'tensor', [(dev, (dev + 1) % 4) for dev in range(4)])]
    all_gather x1, waiting for transfers between devices: 71.6 us -> 43.2 us  [on_device(): lax.all_gather(shared_down, 'dp', axis=1, tiled=True)]
    all_to_all x1, blocking collectives: 13.3 us -> 20.2 us  [on_device(): lax.all_to_all(to_send, 'dp', split_axis=0, concat_axis=0, tiled=True)]
    all_gather x1, waiting for transfers between devices: 66 us -> 71.6 us  [on_device(): lax.all_gather(shared_up, 'dp', axis=0, tiled=True)]
  transfers between devices with their start and end apart: 7 -> 9, of which waited for: 7 -> 8; matrix products, arithmetic and copies ran while one was open for 8% -> 12% of each run, Pallas kernels for 0% -> 0%
where the time goes in v1:
time: 362 us
  waiting for transfers between devices  264 us (73%)
  blocking collectives  33.9 us (9%)
  matrix products  31.1 us (9%)
  local copies, waits for them, and re-layouts  15.9 us (4%)
  between operations  13.7 us (4%)
    all_gather x1, waiting for transfers between devices, on_device(): lax.all_gather(shared_up, 'dp', axis=0, tiled=True)  71.6 us
    ppermute x3, waiting for transfers between devices, on_device(): lax.ppermute(ring[-1], 'tensor', [(dev, (dev + 1) % 4) for dev in range(4)])  51.1 us
    all_gather x1, waiting for transfers between devices, on_device(): lax.all_gather(shared_down, 'dp', axis=1, tiled=True)  43.2 us
    reduce_scatter x1, waiting for transfers between devices, on_device(): lax.psum_scatter(expert_terms.astype(jnp.bfloat16), 'tensor', scatter_dim...  43.2 us
    all_gather x1, waiting for transfers between devices, on_device(): gathered = lax.all_gather(tokens, 'tensor', axis=1, tiled=True)  34.8 us
    all_to_all x1, blocking collectives, on_device(): lax.all_to_all(to_send, 'dp', split_axis=0, concat_axis=0, tiled=True)  20.2 us
    reduce_scatter x1, waiting for transfers between devices, on_device(): lax.psum_scatter(shared_terms.astype(jnp.bfloat16), 'tensor', scatter_dim...  17.5 us
    all_to_all x1, blocking collectives, on_device(): lax.all_to_all(lax.psum_scatter(expert_terms.astype(jnp.bfloat16), 'tenso...  13.7 us
  transfers between devices with their start and end apart: 9, of which 8 were waited for; matrix products, arithmetic and copies ran while one was open for 12% of the time, Pallas kernels for 0%

profile of v1, /device:TPU:0, one launch (start us, length us, event | category | flops | bytes accessed | tf_op | source)
XLA Modules:
  0.0 361.7 jit_solution(17305012003805012366)
XLA Ops:
  6.6 0.7 all-gather.5.cloned.1.call-update
  7.3 0.7 all-gather.7.cloned.1.call-update
  8.1 0.7 all-gather.11.cloned.1.call-update
  8.8 0.5 all-gather.9.cloned.1.call-update
  9.4 34.8 %all-gather.5.cloned.1.call-done = bf16[128,5120]{1,0:T(8,128)(2,1)} async-done(((bf16[128,1280]{1,0:T(8,128)(2,1)}), bf16[128,5120]{1,0:T(8,128)(2,1)}) %all-gather.5.cloned.1.call-update) | async-done | bytes 1310736 | tf_op jit(solution)/shard_map/all_gather | solution.py:23
  44.2 1.8 fusion.2
  46.0 0.1 multiply_convert_fusion
  46.2 9.8 %scatter_fusion = bf16[2,64,1280]{2,1,0:T(8,128)(2,1)S(1)} fusion(bf16[2,64,1280]{2,1,0:T(8,128)(2,1)S(1)} %broadcast_in_dim.8, s32[128]{0:T(128)S(1)} %get-tuple-element.6, bf16[128,1280]{1,0:T(8,128)(2,1)S(1)} %multiply_convert_fusion), kind=kCustom, calls=%fused_computation.1 | custom fusion | bytes 984064 | tf_op jit(solution)/shard_map/scatter | solution.py:33
  56.1 20.2 %all_to_all.10 = bf16[4,64,1280]{2,1,0:T(8,128)(2,1)S(1)} all-to-all(bf16[4,64,1280]{2,1,0:T(8,128)(2,1)S(1)} %bitcast.44), channel_id=1, replica_groups=mesh['group'=2,'dp'=4,'tensor'=4] {'dp'}, dimensions={0} | all-to-all | bytes 1310720 | tf_op jit(solution)/shard_map/all_to_all | solution.py:55
  76.3 1.0 collective-permute-start
  77.3 17.2 %collective-permute-done = bf16[4,64,1280]{2,1,0:T(8,128)(2,1)S(1)} collective-permute-done((bf16[4,64,1280]{2,1,0:T(8,128)(2,1)S(1)}, bf16[4,64,1280]{2,1,0:T(8,128)(2,1)S(1)}, u32[]{:S(2)}, u32[]{:S(2)}) %collective-permute-start) | collective-permute-done | bytes 655392 | tf_op jit(solution)/shard_map/ppermute | solution.py:61
  94.5 17.4 %collective-permute-done.1 = bf16[4,64,1280]{2,1,0:T(8,128)(2,1)S(1)} collective-permute-done((bf16[4,64,1280]{2,1,0:T(8,128)(2,1)S(1)}, bf16[4,64,1280]{2,1,0:T(8,128)(2,1)S(1)}, u32[]{:S(2)}, u32[]{:S(2)}) %collective-permute-start.1) | collective-permute-done | bytes 655392 | tf_op jit(solution)/shard_map/ppermute | solution.py:61
  111.8 16.5 %collective-permute-done.2 = bf16[4,64,1280]{2,1,0:T(8,128)(2,1)S(1)} collective-permute-done((bf16[4,64,1280]{2,1,0:T(8,128)(2,1)S(1)}, bf16[4,64,1280]{2,1,0:T(8,128)(2,1)S(1)}, u32[]{:S(2)}, u32[]{:S(2)}) %collective-permute-start.2) | collective-permute-done | bytes 655392 | tf_op jit(solution)/shard_map/ppermute | solution.py:61
  128.4 0.1 constant_dynamic-update-slice_fusion.6
  128.5 0.1 constant_dynamic-update-slice_fusion.5
  128.6 0.1 constant_dynamic-update-slice_fusion.4
  128.8 0.1 constant_dynamic-update-slice_fusion.1
  129.0 1.0 constant_dynamic-slice_fusion
  130.0 1.5 copy-done.3
  131.5 1.0 slice-done.1
  132.5 1.5 fusion.23
  134.0 11.0 %convolution_convert_fusion = bf16[256,5120]{1,0:T(8,128)(2,1)} fusion(bf16[512,5120]{1,0:T(8,128)(2,1)} %param.14, bf16[256,5120]{1,0:T(8,128)(2,1)} %bitcast.43, bf16[5120,512]{1,0:T(8,128)(2,1)} %param.13, f32[256,512]{1,0:T(8,128)S(1)} %fusion.23), kind=kOutput, calls=%fused_computation.2 | convolution fusion | flops 2686451712 | bytes 16252928 | tf_op jit(solution)/shard_map/dot_general | solution.py:71
  145.1 5.6 %fusion.22 = f32[128,1024]{1,0:T(8,128)S(1)} fusion(bf16[128,5120]{1,0:T(8,128)(2,1)S(1)} %copy-done.2, bf16[5120,1024]{1,0:T(8,128)(2,1)} %all-gather.7.cloned.1.call-done), kind=kOutput, calls=%fused_computation.47 | convolution fusion | flops 1342177280 | bytes 12320768 | tf_op jit(solution)/shard_map/dot_general | solution.py:35
  150.7 43.2 %all-gather.11.cloned.1.call-done = bf16[1024,5120]{1,0:T(8,128)(2,1)} async-done(((bf16[1024,1280]{1,0:T(8,128)(2,1)}), bf16[1024,5120]{1,0:T(8,128)(2,1)}) %all-gather.11.cloned.1.call-update) | async-done | bytes 10485776 | tf_op jit(solution)/shard_map/all_gather | solution.py:48
  193.9 71.6 %all-gather.9.cloned.1.call-done = bf16[5120,1024]{1,0:T(8,128)(2,1)} async-done(((bf16[1280,1024]{1,0:T(8,128)(2,1)}), bf16[5120,1024]{1,0:T(8,128)(2,1)}) %all-gather.9.cloned.1.call-update) | async-done | bytes 10485776 | tf_op jit(solution)/shard_map/all_gather | solution.py:42
  265.5 11.2 %convolution_convert_fusion.1 = bf16[128,5120]{1,0:T(8,128)(2,1)} fusion(bf16[1024,5120]{1,0:T(8,128)(2,1)} %all-gather.11.cloned.1.call-done, bf16[128,5120]{1,0:T(8,128)(2,1)S(1)} %copy-done.2, bf16[5120,1024]{1,0:T(8,128)(2,1)} %all-gather.9.cloned.1.call-done, f32[128,1024]{1,0:T(8,128)S(1)} %fusion.22), kind=kOutput, calls=%fused_computation.3 | convolution fusion | flops 2685796352 | bytes 24117248 | tf_op jit(solution)/shard_map/dot_general | solution.py:46
  276.7 43.2 %reduce-scatter.5.cloned.1.call-done = bf16[4,64,1280]{2,1,0:T(8,128)(2,1)} async-done(((bf16[4,64,5120]{2,1,0:T(8,128)(2,1)}), bf16[4,64,1280]{2,1,0:T(8,128)(2,1)}) %reduce-scatter.5.cloned.1.call-update) | async-done | bytes 655376 | tf_op jit(solution)/shard_map/reduce_scatter | solution.py:74
  319.9 13.7 %all_to_all.11 = bf16[4,64,1280]{2,1,0:T(8,128)(2,1)S(1)} all-to-all(bf16[4,64,1280]{2,1,0:T(8,128)(2,1)} %reduce-scatter.5.cloned.1.call-done), channel_id=1, replica_groups=mesh['group'=2,'dp'=4,'tensor'=4] {'dp'}, dimensions={0} | all-to-all | bytes 1310720 | tf_op jit(solution)/shard_map/all_to_all | solution.py:73
  333.6 0.1 bitcast_reduce_fusion
  333.7 1.9 gather_fusion
  335.6 17.5 %reduce-scatter.3.cloned.1.call-done = bf16[128,1280]{1,0:T(8,128)(2,1)} async-done(((bf16[128,5120]{1,0:T(8,128)(2,1)}), bf16[128,1280]{1,0:T(8,128)(2,1)}) %reduce-scatter.3.cloned.1.call-update) | async-done | bytes 327696 | tf_op jit(solution)/shard_map/reduce_scatter | solution.py:51
  353.0 1.8 add_convert_fusion
  (36 shorter events, 0.7 us)
Async XLA Ops:
  6.5 37.7 %copy-start = (bf16[5120,2]{0,1:T(2,128)(2,1)S(1)}, bf16[5120,2]{0,1:T(2,128)(2,1)}, u32[]{:S(2)}) copy-start(bf16[5120,2]{0,1:T(2,128)(2,1)} %param.11) | copy-start | bytes 61444
  6.5 39.4 %copy-start.4 = (bf16[128,1280]{1,0:T(8,128)(2,1)S(1)}, bf16[128,1280]{1,0:T(8,128)(2,1)}, u32[]{:S(2)}) copy-start(bf16[128,1280]{1,0:T(8,128)(2,1)} %param.10) | copy-start | bytes 983044
  6.5 2.8 copy-start.5
  6.5 2.9 copy-start.6
  6.5 37.6 %all-gather.5.cloned.1.call-start = ((), (), s32[]{:S(2)}) async-start(), calls=%async_computation.4 | async-start | bytes 1638400 | tf_op jit(solution)/shard_map/all_gather | solution.py:23
  7.3 137.8 %all-gather.7.cloned.1.call-start = ((), (), s32[]{:S(2)}) async-start(), calls=%async_computation.5 | async-start | bytes 13107200 | tf_op jit(solution)/shard_map/all_gather | solution.py:37
  8.0 185.8 %all-gather.11.cloned.1.call-start = ((), (), s32[]{:S(2)}) async-start(), calls=%async_computation.7 | async-start | bytes 13107200 | tf_op jit(solution)/shard_map/all_gather | solution.py:48
  8.8 256.7 %all-gather.9.cloned.1.call-start = ((), (), s32[]{:S(2)}) async-start(), calls=%async_computation.6 | async-start | bytes 13107200 | tf_op jit(solution)/shard_map/all_gather | solution.py:42
  9.3 310.6 %reduce-scatter.5.cloned.1.call-start = ((), (), s32[]{:S(2)}) async-start(), calls=%async_computation.9 | async-start | bytes 3276800 | tf_op jit(solution)/shard_map/reduce_scatter | solution.py:74
  76.3 18.2 %collective-permute-start = (bf16[4,64,1280]{2,1,0:T(8,128)(2,1)S(1)}, bf16[4,64,1280]{2,1,0:T(8,128)(2,1)S(1)}, u32[]{:S(2)}, u32[]{:S(2)}) collective-permute-start(bf16[4,64,1280]{2,1,0:T(8,128)(2,1)S(1)} %all_to_all.10), channel_id=1, source_target_pairs={{0,1},{1,2},{2,3},{3,0},{4,5},{5,6},{6,7},{7,4},{8,9},{9,10},{10,1... | collective-permute-start | bytes 1966088 | tf_op jit(solution)/shard_map/ppermute | solution.py:61
  94.5 17.4 %collective-permute-start.1 = (bf16[4,64,1280]{2,1,0:T(8,128)(2,1)S(1)}, bf16[4,64,1280]{2,1,0:T(8,128)(2,1)S(1)}, u32[]{:S(2)}, u32[]{:S(2)}) collective-permute-start(bf16[4,64,1280]{2,1,0:T(8,128)(2,1)S(1)} %collective-permute-done), channel_id=1, source_target_pairs={{0,1},{1,2},{2,3},{3,0},{4,5},{5,6},{6,7},{7,4},{8,9},{9,10},{10,1... | collective-permute-start | bytes 1966088 | tf_op jit(solution)/shard_map/ppermute | solution.py:61
  111.8 16.5 %collective-permute-start.2 = (bf16[4,64,1280]{2,1,0:T(8,128)(2,1)S(1)}, bf16[4,64,1280]{2,1,0:T(8,128)(2,1)S(1)}, u32[]{:S(2)}, u32[]{:S(2)}) collective-permute-start(bf16[4,64,1280]{2,1,0:T(8,128)(2,1)S(1)} %collective-permute-done.1), channel_id=1, source_target_pairs={{0,1},{1,2},{2,3},{3,0},{4,5},{5,6},{6,7},{7,4},{8,9},{9,10},{10,1... | collective-permute-start | bytes 1966088 | tf_op jit(solution)/shard_map/ppermute | solution.py:61
  128.4 3.1 slice-start
  128.8 3.6 %slice-start.1 = ((s8[5242880]{0:T(1024)(128)(4,1)}), s8[1048576]{0:T(1024)(128)(4,1)S(1)}, s32[]{:S(2)}) async-start(s8[5242880]{0:T(1024)(128)(4,1)} %bitcast.45), calls=%async_computation.11 | async-start | bytes 2097152
  130.0 1.5 copy-start.3
  134.0 11.1 %copy-start.2 = (bf16[128,5120]{1,0:T(8,128)(2,1)S(1)}, bf16[128,5120]{1,0:T(8,128)(2,1)}, u32[]{:S(2)}) copy-start(bf16[128,5120]{1,0:T(8,128)(2,1)} %all-gather.5.cloned.1.call-done) | copy-start | bytes 3932164
  145.0 208.1 %reduce-scatter.3.cloned.1.call-start = ((), (), s32[]{:S(2)}) async-start(), calls=%async_computation.8 | async-start | bytes 1638400 | tf_op jit(solution)/shard_map/reduce_scatter | solution.py:51
  265.5 89.4 %copy-start.1 = (bf16[5120,2]{0,1:T(2,128)(2,1)S(1)}, bf16[5120,2]{0,1:T(2,128)(2,1)}, u32[]{:S(2)}) copy-start(bf16[5120,2]{0,1:T(2,128)(2,1)} %param.11) | copy-start | bytes 61444
Sparse Core Ops, SparseCore 0:
  8.9 35.2 all-gather.4
  45.7 76.2 all-gather.6
  123.7 70.1 all-gather.10
  195.3 70.1 all-gather.8
  267.6 52.2 reduce-scatter.4
  322.1 30.9 reduce-scatter.2
